TPU v7x, 32 devices: a whole 2x2x4 slice. The times are simulated.
32 devices in a mesh: wide: 16 (over z, x, core), narrow: 2 (over y).
Axes of the slice: x: 2, y: 2, z: 4, core: 2. Of those that a mesh axis runs over, the one named last changes fastest.
Arguments:
- vectors: float32 [1024, 16384], P('narrow', 'wide'), may hold values from -6 to 6
- weights: bfloat16 [5, 64, 256, 512], P(None, 'wide', 'narrow'), may hold values from -0.25 to 0.25
Outputs:
- transformed: float32 [1024, 16384], P('narrow', 'wide')
All inputs are finite; a program needn't handle non-finite values.
Results may differ from a plain program's by a relative error of at most 0.0003.
Values may be sent and summed in bfloat16 or wider, within the bound.
A program may use at most 64 MiB of HBM per device.

v0:
```python
import jax
import jax.numpy as jnp
from jax import lax
from jax.sharding import PartitionSpec as P


def swapped(shard, axis, apart):
    return lax.ppermute(shard, axis, [(i, i ^ 1 << apart) for i in range(lax.axis_size(axis))])


def pair_local(current, level_bit):
    columns, block_count, block_size = current.shape
    stride = 1 << level_bit
    grouped = current.reshape(columns, block_count // (2 * stride), 2, stride, block_size)
    paired = jnp.concatenate([grouped[:, :, 0], grouped[:, :, 1]], -1)
    spread = jnp.broadcast_to(
        paired[:, :, None], (columns, block_count // (2 * stride), 2, stride, 2 * block_size)
    )
    return spread.reshape(columns, block_count, 2 * block_size)


def upper_side(level_bit):
    return lax.axis_index("wide") // (1 << level_bit) % 2


def pair_wide(current, level_bit):
    partner = swapped(current, "wide", level_bit)
    upper_bit = upper_side(level_bit)
    lower_half = jnp.where(upper_bit == 1, partner, current)
    upper_half = jnp.where(upper_bit == 1, current, partner)
    return jnp.concatenate([lower_half, upper_half], -1)


def contract(paired, matrix_rows):
    return jnp.einsum(
        "cbi,boi->cbo", paired, matrix_rows.astype(jnp.float32), precision=lax.Precision.HIGHEST
    )


def gathered_level(paired, level_weight):
    return contract(paired, lax.all_gather(level_weight, "narrow", axis=1, tiled=True))


def on_device(vectors, weights):
    columns, coeffs = vectors.shape
    block_size = weights.shape[3] // 2
    current = vectors.reshape(columns, coeffs // block_size, block_size)
    wide_top = lax.axis_size("wide").bit_length() - 1
    wide_bits = [0, wide_top // 2, wide_top - 1]
    for level_index in range(5):
        if level_index < 2:
            paired = pair_local(current, level_index)
            current = gathered_level(paired, weights[level_index])
        else:
            paired = pair_wide(current, wide_bits[level_index - 2])
            current = gathered_level(paired, weights[level_index])
    return current.reshape(columns, coeffs)


def solution(mesh):
    placed = (P("narrow", "wide"), P(None, "wide", "narrow", None))
    return jax.shard_map(
        on_device, mesh=mesh, in_specs=placed, out_specs=P("narrow", "wide"), check_vma=False
    )
```

profile of v0, /device:TPU:0, one launch (start us, length us, event | category | flops | bytes accessed | tf_op | source)
XLA Modules:
  0.0 252.6 jit_solution(388550160827460083)
XLA Ops:
  6.5 0.0 all-gather.11.cloned.1.call-start
  6.5 3.2 %fusion.27 = (bf16[1,4,128,512]{3,2,1,0:T(8,128)(2,1)}, bf16[1,4,128,512]{3,2,1,0:T(8,128)(2,1)}, bf16[1,4,128,512]{3,2,1,0:T(8,128)(2,1)}, bf16[1,4,128,512]{3,2,1,0:T(8,128)(2,1)}, bf16[1,4,128,512]{3,2,1,0:T(8,128)(2,1)}) fusion(bf16[5,4,128,512]{3,2,1,0:T(8,128)(2,1)} %param.3), kind=kLoop, calls=%fused_computation.37 | loop fusion | bytes 5242880 | tf_op jit(solution)/shard_map/slice | solution.py:56
  9.8 0.0 all-gather.11.cloned.1.call-update
  9.8 0.0 all-gather.13.cloned.1.call-start
  9.8 0.7 all-gather.13.cloned.1.call-update
  10.5 0.0 all-gather.15.cloned.1.call-start
  10.6 3.0 %reshape_reshape.3 = f32[512,2,2,1,256]{4,2,1,0,3:T(2,128)S(1)} reshape(f32[512,1024]{1,0:T(8,128)} %param.2) | data formatting | bytes 4194304 | tf_op jit(solution)/shard_map/reshape;reshape | solution.py:14
  13.6 1.1 slice_bitcast_fusion.2
  14.7 0.7 slice_bitcast_fusion.3
  15.4 1.8 pad_maximum_fusion
  17.2 0.4 copy.15
  17.7 16.3 %all-gather.11.cloned.1.call-done = bf16[1,4,256,512]{3,2,1,0:T(8,128)(2,1)} async-done(((bf16[1,4,128,512]{3,2,1,0:T(8,128)(2,1)}), bf16[1,4,256,512]{3,2,1,0:T(8,128)(2,1)}) %all-gather.11.cloned.1.call-update) | async-done | bytes 1048592 | tf_op jit(solution)/shard_map/all_gather | solution.py:41
  33.9 0.0 copy-start.1
  33.9 0.6 broadcast_in_dim.21
  34.6 0.6 copy-done.1
  35.2 2.3 fusion.22
  37.4 0.2 slice_bitcast_fusion.1
  37.6 1.5 maximum_bitcast_fusion
  39.1 1.9 copy.5
  41.0 15.7 %all-gather.13.cloned.1.call-done = bf16[1,4,256,512]{3,2,1,0:T(8,128)(2,1)} async-done(((bf16[1,4,128,512]{3,2,1,0:T(8,128)(2,1)}), bf16[1,4,256,512]{3,2,1,0:T(8,128)(2,1)}) %all-gather.13.cloned.1.call-update) | async-done | bytes 1048592 | tf_op jit(solution)/shard_map/all_gather | solution.py:41
  56.8 0.0 copy-start
  56.8 0.6 broadcast_in_dim.24
  57.4 0.6 copy-done
  58.0 2.3 convolution_bitcast_fusion
  60.3 0.1 collective-permute-start
  60.4 0.0 all-gather.15.cloned.1.call-update
  60.4 0.2 all-gather.17.cloned.1.call-start
  60.7 4.0 %collective-permute-done = f32[512,4,256]{0,2,1:T(8,128)} collective-permute-done((f32[512,4,256]{0,2,1:T(8,128)S(1)}, f32[512,4,256]{0,2,1:T(8,128)}, u32[]{:S(2)}, u32[]{:S(2)}) %collective-permute-start) | collective-permute-done | bytes 2097184 | tf_op jit(solution)/shard_map/ppermute | solution.py:8
  64.7 4.4 %broadcast_select_fusion.1 = (f32[512,4,256]{0,2,1:T(8,128)}, f32[512,4,256]{0,2,1:T(8,128)}) fusion(f32[512,4,256]{0,2,1:T(8,128)} %collective-permute-done, f32[512,4,256]{0,2,1:T(8,128)S(1)} %convolution_bitcast_fusion, pred[]{:T(512)S(6)} %eq.18), kind=kLoop, calls=%fused_computation.29 | loop fusion | flops 1048576 | bytes 8388609 | tf_op jit(solution)/shard_map/jit(_where)/select_n | solution.py:29
  69.0 13.0 %all-gather.15.cloned.1.call-done = bf16[1,4,256,512]{3,2,1,0:T(8,128)(2,1)} async-done(((bf16[1,4,128,512]{3,2,1,0:T(8,128)(2,1)}), bf16[1,4,256,512]{3,2,1,0:T(8,128)(2,1)}) %all-gather.15.cloned.1.call-update) | async-done | bytes 1048592 | tf_op jit(solution)/shard_map/all_gather | solution.py:41
  82.0 4.6 %fusion.15 = f32[512,4,256]{0,2,1:T(8,128)S(1)} fusion(f32[512,4,256]{0,2,1:T(8,128)} %get-tuple-element.10, f32[512,4,256]{0,2,1:T(8,128)} %get-tuple-element.9, bf16[1,4,256,512]{3,2,1,0:T(8,128)(2,1)} %all-gather.15.cloned.1.call-done), kind=kOutput, calls=%fused_computation.16 | convolution fusion | flops 3222274048 | bytes 7340032 | tf_op jit(solution)/shard_map/cbi,boi->cbo/dot_general | solution.py:35
  86.6 1.6 collective-permute-start.1
  88.2 0.0 all-gather.17.cloned.1.call-update
  88.2 0.0 all-gather.19.cloned.1.call-start
  88.3 45.7 %collective-permute-done.1 = f32[512,4,256]{0,2,1:T(8,128)} collective-permute-done((f32[512,4,256]{0,2,1:T(8,128)S(1)}, f32[512,4,256]{0,2,1:T(8,128)}, u32[]{:S(2)}, u32[]{:S(2)}) %collective-permute-start.1) | collective-permute-done | bytes 2097184 | tf_op jit(solution)/shard_map/ppermute | solution.py:8
  134.0 4.4 %broadcast_select_fusion.3 = (f32[512,4,256]{0,2,1:T(8,128)}, f32[512,4,256]{0,2,1:T(8,128)}) fusion(f32[512,4,256]{0,2,1:T(8,128)} %collective-permute-done.1, f32[512,4,256]{0,2,1:T(8,128)S(1)} %fusion.15, pred[]{:T(512)S(6)} %eq.17), kind=kLoop, calls=%fused_computation.31 | loop fusion | flops 1048576 | bytes 8388609 | tf_op jit(solution)/shard_map/jit(_where)/select_n | solution.py:29
  138.3 0.0 all-gather.17.cloned.1.call-done
  138.3 4.6 %fusion.12 = f32[512,4,256]{0,2,1:T(8,128)S(1)} fusion(f32[512,4,256]{0,2,1:T(8,128)} %get-tuple-element.8, f32[512,4,256]{0,2,1:T(8,128)} %get-tuple-element.7, bf16[1,4,256,512]{3,2,1,0:T(8,128)(2,1)} %all-gather.17.cloned.1.call-done), kind=kOutput, calls=%fused_computation.15 | convolution fusion | flops 3222274048 | bytes 7340032 | tf_op jit(solution)/shard_map/cbi,boi->cbo/dot_general | solution.py:35
  143.0 2.5 collective-permute-start.2
  145.4 0.0 all-gather.19.cloned.1.call-update
  145.5 89.8 %collective-permute-done.2 = f32[512,4,256]{0,2,1:T(8,128)} collective-permute-done((f32[512,4,256]{0,2,1:T(8,128)S(1)}, f32[512,4,256]{0,2,1:T(8,128)}, u32[]{:S(2)}, u32[]{:S(2)}) %collective-permute-start.2) | collective-permute-done | bytes 2097184 | tf_op jit(solution)/shard_map/ppermute | solution.py:8
  235.3 4.4 %broadcast_select_fusion.5 = (f32[512,4,256]{0,2,1:T(8,128)}, f32[512,4,256]{0,2,1:T(8,128)}) fusion(f32[512,4,256]{0,2,1:T(8,128)} %collective-permute-done.2, f32[512,4,256]{0,2,1:T(8,128)S(1)} %fusion.12, pred[]{:T(512)S(6)} %eq.16), kind=kLoop, calls=%fused_computation.33 | loop fusion | flops 1048576 | bytes 8388609 | tf_op jit(solution)/shard_map/jit(_where)/select_n | solution.py:29
  239.7 0.0 all-gather.19.cloned.1.call-done
  239.7 4.6 %fusion.8 = f32[4,512,256]{1,2,0:T(8,128)S(1)} fusion(f32[512,4,256]{0,2,1:T(8,128)} %get-tuple-element.6, f32[512,4,256]{0,2,1:T(8,128)} %get-tuple-element.5, bf16[1,4,256,512]{3,2,1,0:T(8,128)(2,1)} %all-gather.19.cloned.1.call-done), kind=kOutput, calls=%fused_computation.8 | convolution fusion | flops 3222274048 | bytes 7340032 | tf_op jit(solution)/shard_map/cbi,boi->cbo/dot_general | solution.py:35
  244.3 1.8 copy.9
Async XLA Ops:
  6.5 27.4 %all-gather.11.cloned.1.call-start = ((), (), s32[]{:S(2)}) async-start(), calls=%async_computation | async-start | bytes 1572864 | tf_op jit(solution)/shard_map/all_gather | solution.py:41
  9.8 47.0 %all-gather.13.cloned.1.call-start = ((), (), s32[]{:S(2)}) async-start(), calls=%async_computation.1 | async-start | bytes 1572864 | tf_op jit(solution)/shard_map/all_gather | solution.py:41
  10.5 71.5 %all-gather.15.cloned.1.call-start = ((), (), s32[]{:S(2)}) async-start(), calls=%async_computation.2 | async-start | bytes 1572864 | tf_op jit(solution)/shard_map/all_gather | solution.py:41
  33.9 1.2 copy-start.1
  56.8 1.2 copy-start
  60.3 4.4 %collective-permute-start = (f32[512,4,256]{0,2,1:T(8,128)S(1)}, f32[512,4,256]{0,2,1:T(8,128)}, u32[]{:S(2)}, u32[]{:S(2)}) collective-permute-start(f32[512,4,256]{0,2,1:T(8,128)S(1)} %convolution_bitcast_fusion), channel_id=1, source_target_pairs={{0,2},{2,0},{4,6},{6,4},{8,10},{10,8},{12,14},{14,12},{16,18},{18,... | collective-permute-start | bytes 6291464 | tf_op jit(solution)/shard_map/ppermute | solution.py:8
  60.4 77.9 %all-gather.17.cloned.1.call-start = ((), (), s32[]{:S(2)}) async-start(), calls=%async_computation.3 | async-start | bytes 1572864 | tf_op jit(solution)/shard_map/all_gather | solution.py:41
  86.6 47.4 %collective-permute-start.1 = (f32[512,4,256]{0,2,1:T(8,128)S(1)}, f32[512,4,256]{0,2,1:T(8,128)}, u32[]{:S(2)}, u32[]{:S(2)}) collective-permute-start(f32[512,4,256]{0,2,1:T(8,128)S(1)} %fusion.15), channel_id=1, source_target_pairs={{0,8},{2,10},{4,12},{6,14},{8,0},{10,2},{12,4},{14,6},{16,24},{18,... | collective-permute-start | bytes 6291464 | tf_op jit(solution)/shard_map/ppermute | solution.py:8
  88.2 151.5 %all-gather.19.cloned.1.call-start = ((), (), s32[]{:S(2)}) async-start(), calls=%async_computation.4 | async-start | bytes 1572864 | tf_op jit(solution)/shard_map/all_gather | solution.py:41
  143.0 92.4 %collective-permute-start.2 = (f32[512,4,256]{0,2,1:T(8,128)S(1)}, f32[512,4,256]{0,2,1:T(8,128)}, u32[]{:S(2)}, u32[]{:S(2)}) collective-permute-start(f32[512,4,256]{0,2,1:T(8,128)S(1)} %fusion.12), channel_id=1, source_target_pairs={{0,16},{2,18},{4,20},{6,22},{8,24},{10,26},{12,28},{14,30},{16,0},... | collective-permute-start | bytes 6291464 | tf_op jit(solution)/shard_map/ppermute | solution.py:8
Sparse Core Ops, SparseCore 0:
  9.9 23.9 all-gather.10
  35.5 21.2 all-gather.12
  60.5 21.4 all-gather.14
  88.3 20.3 all-gather.16
  145.6 19.4 all-gather.18
where the time goes:
time: 253 us
  waiting for transfers between devices  185 us (73%)
  matrix products  18.4 us (7%)
  other arithmetic  16.3 us (6%)
  local copies, waits for them, and re-layouts  14.8 us (6%)
  between operations  13.3 us (5%)
  starting transfers between devices  4.44 us (2%)
    ppermute x3, waiting for transfers between devices, swapped(): lax.ppermute(shard, axis, [(i, i ^ 1 << apart) for i in range(lax.axis_si...  140 us
    all_gather x5, waiting for transfers between devices, gathered_level(): lax.all_gather(level_weight, 'narrow', axis=1, tiled=True)  45 us
    dot_general x5, matrix products, contract(): jnp.einsum('cbi,boi->cbo', paired, matrix_rows.astype(jnp.float32), preci...  18.4 us
    select_n x3, other arithmetic, pair_wide(): lower_half = jnp.where(upper_bit == 1, partner, current)  13.1 us
  transfers between devices with their start and end apart: 8, of which 6 were waited for; matrix products, arithmetic and copies ran while one was open for 11% of the time, Pallas kernels for 0%

commit v1 on v0

--- a/solution.py
+++ b/solution.py
@@ -38,7 +38,13 @@
 
 
 def gathered_level(paired, level_weight):
-    return contract(paired, lax.all_gather(level_weight, "narrow", axis=1, tiled=True))
+    return contract(
+        paired,
+        jnp.concatenate(
+            lax.all_to_all(jnp.stack([level_weight] * lax.axis_size("narrow")), "narrow", 0, 0),
+            axis=1,
+        ),
+    )
 
 
 def on_device(vectors, weights):

time: 253 us -> 219 us (0.87)
  waiting for transfers between devices: 185 us -> 152 us
  starting transfers between devices: 4.44 us -> 23 us
  between operations: 13.3 us -> 0.33 us
  matrix products: 18.4 us -> 10.8 us
    all_to_all x0 -> x5, waiting for transfers between devices: none -> 51.6 us  [gathered_level(): lax.all_to_all(jnp.stack([level_weight] * lax.axis_size('narrow')), 'narr...]
    all_gather x5 -> x0, waiting for transfers between devices: 45 us -> none  [gathered_level(): lax.all_gather(level_weight, 'narrow', axis=1, tiled=True)]
    ppermute x3, waiting for transfers between devices: 140 us -> 100 us  [swapped(): lax.ppermute(shard, axis, [(i, i ^ 1 << apart) for i in range(lax.axis_si...]
    all_to_all x0 -> x5, starting transfers between devices: none -> 18.8 us  [gathered_level(): lax.all_to_all(jnp.stack([level_weight] * lax.axis_size('narrow')), 'narr...]
    dot_general x5, matrix products: 18.4 us -> 10.8 us  [contract(): jnp.einsum('cbi,boi->cbo', paired, matrix_rows.astype(jnp.float32), preci...]
    select_n x3, other arithmetic: 13.1 us -> 6.77 us  [pair_wide(): lower_half = jnp.where(upper_bit == 1, partner, current)]
    another operation x0 -> x5, other arithmetic: none -> 5.31 us  [gathered_level(): jnp.stack([level_weight] * lax.axis_size('narrow'))]
  transfers between devices with their start and end apart: 8 -> 8, of which waited for: 6 -> 7; matrix products, arithmetic and copies ran while one was open for 11% -> 9% of each run, Pallas kernels for 0% -> 0%
where the time goes in v1:
time: 219 us; the launch traced here: 218 us
  waiting for transfers between devices  152 us (69%)
  starting transfers between devices  23 us (11%)
  local copies, waits for them, and re-layouts  16.5 us (8%)
  other arithmetic  15.4 us (7%)
  matrix products  10.8 us (5%)
    ppermute x3, waiting for transfers between devices, swapped(): lax.ppermute(shard, axis, [(i, i ^ 1 << apart) for i in range(lax.axis_si...  100 us
    all_to_all x5, waiting for transfers between devices, gathered_level(): lax.all_to_all(jnp.stack([level_weight] * lax.axis_size('narrow')), 'narr...  51.6 us
    all_to_all x5, starting transfers between devices, gathered_level(): lax.all_to_all(jnp.stack([level_weight] * lax.axis_size('narrow')), 'narr...  18.8 us
    dot_general x5, matrix products, contract(): jnp.einsum('cbi,boi->cbo', paired, matrix_rows.astype(jnp.float32), preci...  10.8 us
    select_n x3, other arithmetic, pair_wide(): lower_half = jnp.where(upper_bit == 1, partner, current)  6.77 us
    another operation x5, other arithmetic, gathered_level(): jnp.stack([level_weight] * lax.axis_size('narrow'))  5.31 us
  transfers between devices with their start and end apart: 8, of which 7 were waited for; matrix products, arithmetic and copies ran while one was open for 9% of the time, Pallas kernels for 0%

profile of v1, /device:TPU:0, one launch (start us, length us, event | category | flops | bytes accessed | tf_op | source)
XLA Modules:
  0.0 217.8 jit_solution(12329616684793876451)
XLA Ops:
  0.0 3.1 %fusion.21 = (bf16[1,4,128,512]{3,2,1,0:T(8,128)(2,1)S(1)}, bf16[1,4,128,512]{3,2,1,0:T(8,128)(2,1)}, bf16[1,4,128,512]{3,2,1,0:T(8,128)(2,1)}, bf16[1,4,128,512]{3,2,1,0:T(8,128)(2,1)}, bf16[1,4,128,512]{3,2,1,0:T(8,128)(2,1)}) fusion(bf16[5,4,128,512]{3,2,1,0:T(8,128)(2,1)} %param.3), kind=kLoop, calls=%fused_computation.36 | loop fusion | bytes 5242880 | tf_op jit(solution)/shard_map/slice | solution.py:59
  3.1 1.1 pad_maximum_fusion.5
  4.1 4.3 %all-to-all-start.4 = ((bf16[2,4,128,512]{3,2,1,0:T(8,128)(2,1)}), bf16[2,4,128,512]{3,2,1,0:T(8,128)(2,1)S(1)}, u32[]{:S(2)}, u32[]{:S(2)}) async-start(bf16[2,4,128,512]{3,2,1,0:T(8,128)(2,1)} %pad_maximum_fusion.5), calls=%async_computation.4 | async-start | bytes 2097152 | tf_op jit(solution)/shard_map/all_to_all | solution.py:44
  8.4 3.0 %reshape_reshape.3 = f32[512,2,2,1,256]{4,2,1,0,3:T(2,128)S(1)} reshape(f32[512,1024]{1,0:T(8,128)} %param.2) | data formatting | bytes 4194304 | tf_op jit(solution)/shard_map/reshape;reshape | solution.py:14
  11.4 1.1 slice_bitcast_fusion.2
  12.5 0.7 slice_bitcast_fusion.3
  13.2 1.8 pad_maximum_fusion
  15.1 0.4 copy.20
  15.5 0.6 copy-done.4
  16.1 1.1 pad_maximum_fusion.4
  17.2 5.6 %all-to-all-done.4 = bf16[2,4,128,512]{3,2,1,0:T(8,128)(2,1)S(1)} async-done(((bf16[2,4,128,512]{3,2,1,0:T(8,128)(2,1)}), bf16[2,4,128,512]{3,2,1,0:T(8,128)(2,1)S(1)}, u32[]{:S(2)}, u32[]{:S(2)}) %all-to-all-start.4) | async-done | bytes 1048608 | tf_op jit(solution)/shard_map/all_to_all | solution.py:44
  22.8 1.0 copy-done
  23.8 3.6 %all-to-all-start.3 = ((bf16[2,4,128,512]{3,2,1,0:T(8,128)(2,1)}), bf16[2,4,128,512]{3,2,1,0:T(8,128)(2,1)S(1)}, u32[]{:S(2)}, u32[]{:S(2)}) async-start(bf16[2,4,128,512]{3,2,1,0:T(8,128)(2,1)} %pad_maximum_fusion.4), calls=%async_computation.3 | async-start | bytes 2097152 | tf_op jit(solution)/shard_map/all_to_all | solution.py:44
  27.4 1.3 copy.7
  28.7 0.5 broadcast_in_dim.21
  29.2 2.2 fusion.22
  31.4 0.2 slice_bitcast_fusion.1
  31.6 1.5 maximum_bitcast_fusion
  33.1 1.9 copy.10
  35.0 5.7 %all-to-all-done.3 = bf16[2,4,128,512]{3,2,1,0:T(8,128)(2,1)S(1)} async-done(((bf16[2,4,128,512]{3,2,1,0:T(8,128)(2,1)}), bf16[2,4,128,512]{3,2,1,0:T(8,128)(2,1)S(1)}, u32[]{:S(2)}, u32[]{:S(2)}) %all-to-all-start.3) | async-done | bytes 1048608 | tf_op jit(solution)/shard_map/all_to_all | solution.py:44
  40.7 0.1 copy.6
  40.7 0.6 broadcast_in_dim.24
  41.3 2.1 convolution_bitcast_fusion
  43.5 0.1 collective-permute-start
  43.6 1.1 pad_maximum_fusion.3
  44.6 3.8 %all-to-all-start.2 = ((bf16[2,4,128,512]{3,2,1,0:T(8,128)(2,1)}), bf16[2,4,128,512]{3,2,1,0:T(8,128)(2,1)S(1)}, u32[]{:S(2)}, u32[]{:S(2)}) async-start(bf16[2,4,128,512]{3,2,1,0:T(8,128)(2,1)} %pad_maximum_fusion.3), calls=%async_computation.2 | async-start | bytes 2097152 | tf_op jit(solution)/shard_map/all_to_all | solution.py:44
  48.4 14.5 %all-to-all-done.2 = bf16[2,4,128,512]{3,2,1,0:T(8,128)(2,1)S(1)} async-done(((bf16[2,4,128,512]{3,2,1,0:T(8,128)(2,1)}), bf16[2,4,128,512]{3,2,1,0:T(8,128)(2,1)S(1)}, u32[]{:S(2)}, u32[]{:S(2)}) %all-to-all-start.2) | async-done | bytes 1048608 | tf_op jit(solution)/shard_map/all_to_all | solution.py:44
  62.9 0.1 copy.5
  63.0 0.0 collective-permute-done
  63.0 2.3 %broadcast_select_fusion.1 = (f32[512,4,256]{0,2,1:T(8,128)S(1)}, f32[512,4,256]{0,2,1:T(8,128)S(1)}) fusion(f32[512,4,256]{0,2,1:T(8,128)} %collective-permute-done, f32[512,4,256]{0,2,1:T(8,128)S(1)} %convolution_bitcast_fusion, pred[]{:T(512)S(6)} %eq.18), kind=kLoop, calls=%fused_computation.28 | loop fusion | flops 1048576 | bytes 8388609 | tf_op jit(solution)/shard_map/jit(_where)/select_n | solution.py:29
  65.3 2.2 fusion.15
  67.4 1.6 collective-permute-start.1
  69.0 1.1 pad_maximum_fusion.2
  70.1 3.6 %all-to-all-start.1 = ((bf16[2,4,128,512]{3,2,1,0:T(8,128)(2,1)}), bf16[2,4,128,512]{3,2,1,0:T(8,128)(2,1)S(1)}, u32[]{:S(2)}, u32[]{:S(2)}) async-start(bf16[2,4,128,512]{3,2,1,0:T(8,128)(2,1)} %pad_maximum_fusion.2), calls=%async_computation.1 | async-start | bytes 2097152 | tf_op jit(solution)/shard_map/all_to_all | solution.py:44
  73.7 13.3 %all-to-all-done.1 = bf16[2,4,128,512]{3,2,1,0:T(8,128)(2,1)S(1)} async-done(((bf16[2,4,128,512]{3,2,1,0:T(8,128)(2,1)}), bf16[2,4,128,512]{3,2,1,0:T(8,128)(2,1)S(1)}, u32[]{:S(2)}, u32[]{:S(2)}) %all-to-all-start.1) | async-done | bytes 1048608 | tf_op jit(solution)/shard_map/all_to_all | solution.py:44
  87.0 0.1 copy.4
  87.1 27.7 %collective-permute-done.1 = f32[512,4,256]{0,2,1:T(8,128)} collective-permute-done((f32[512,4,256]{0,2,1:T(8,128)S(1)}, f32[512,4,256]{0,2,1:T(8,128)}, u32[]{:S(2)}, u32[]{:S(2)}) %collective-permute-start.1) | collective-permute-done | bytes 2097184 | tf_op jit(solution)/shard_map/ppermute | solution.py:8
  114.8 2.3 %broadcast_select_fusion.3 = (f32[512,4,256]{0,2,1:T(8,128)S(1)}, f32[512,4,256]{0,2,1:T(8,128)S(1)}) fusion(f32[512,4,256]{0,2,1:T(8,128)} %collective-permute-done.1, f32[512,4,256]{0,2,1:T(8,128)S(1)} %fusion.15, pred[]{:T(512)S(6)} %eq.17), kind=kLoop, calls=%fused_computation.30 | loop fusion | flops 1048576 | bytes 8388609 | tf_op jit(solution)/shard_map/jit(_where)/select_n | solution.py:29
  117.0 2.2 fusion.12
  119.2 2.6 %collective-permute-start.2 = (f32[512,4,256]{0,2,1:T(8,128)S(1)}, f32[512,4,256]{0,2,1:T(8,128)}, u32[]{:S(2)}, u32[]{:S(2)}) collective-permute-start(f32[512,4,256]{0,2,1:T(8,128)S(1)} %fusion.12), channel_id=1, source_target_pairs={{0,16},{2,18},{4,20},{6,22},{8,24},{10,26},{12,28},{14,30},{16,0},... | collective-permute-start | bytes 6291464 | tf_op jit(solution)/shard_map/ppermute | solution.py:8
  121.8 1.1 pad_maximum_fusion.1
  122.9 3.6 %all-to-all-start = ((bf16[2,4,128,512]{3,2,1,0:T(8,128)(2,1)}), bf16[2,4,128,512]{3,2,1,0:T(8,128)(2,1)S(1)}, u32[]{:S(2)}, u32[]{:S(2)}) async-start(bf16[2,4,128,512]{3,2,1,0:T(8,128)(2,1)} %pad_maximum_fusion.1), calls=%async_computation | async-start | bytes 2097152 | tf_op jit(solution)/shard_map/all_to_all | solution.py:44
  126.5 12.5 %all-to-all-done = bf16[2,4,128,512]{3,2,1,0:T(8,128)(2,1)S(1)} async-done(((bf16[2,4,128,512]{3,2,1,0:T(8,128)(2,1)}), bf16[2,4,128,512]{3,2,1,0:T(8,128)(2,1)S(1)}, u32[]{:S(2)}, u32[]{:S(2)}) %all-to-all-start) | async-done | bytes 1048608 | tf_op jit(solution)/shard_map/all_to_all | solution.py:44
  139.0 0.1 copy.3
  139.0 72.5 %collective-permute-done.2 = f32[512,4,256]{0,2,1:T(8,128)} collective-permute-done((f32[512,4,256]{0,2,1:T(8,128)S(1)}, f32[512,4,256]{0,2,1:T(8,128)}, u32[]{:S(2)}, u32[]{:S(2)}) %collective-permute-start.2) | collective-permute-done | bytes 2097184 | tf_op jit(solution)/shard_map/ppermute | solution.py:8
  211.5 2.3 %broadcast_select_fusion.5 = (f32[512,4,256]{0,2,1:T(8,128)S(1)}, f32[512,4,256]{0,2,1:T(8,128)S(1)}) fusion(f32[512,4,256]{0,2,1:T(8,128)} %collective-permute-done.2, f32[512,4,256]{0,2,1:T(8,128)S(1)} %fusion.12, pred[]{:T(512)S(6)} %eq.16), kind=kLoop, calls=%fused_computation.32 | loop fusion | flops 1048576 | bytes 8388609 | tf_op jit(solution)/shard_map/jit(_where)/select_n | solution.py:29
  213.8 2.2 fusion.8
  216.0 1.8 copy.14
  (8 shorter events, 0.0 us)
Async XLA Ops:
  4.1 18.7 %all-to-all-start.4 = ((bf16[2,4,128,512]{3,2,1,0:T(8,128)(2,1)}), bf16[2,4,128,512]{3,2,1,0:T(8,128)(2,1)S(1)}, u32[]{:S(2)}, u32[]{:S(2)}) async-start(bf16[2,4,128,512]{3,2,1,0:T(8,128)(2,1)} %pad_maximum_fusion.5), calls=%async_computation.4 | async-start | bytes 2097152 | tf_op jit(solution)/shard_map/all_to_all | solution.py:44
  15.1 1.0 copy-start.4
  22.8 1.0 copy-start
  23.8 16.9 %all-to-all-start.3 = ((bf16[2,4,128,512]{3,2,1,0:T(8,128)(2,1)}), bf16[2,4,128,512]{3,2,1,0:T(8,128)(2,1)S(1)}, u32[]{:S(2)}, u32[]{:S(2)}) async-start(bf16[2,4,128,512]{3,2,1,0:T(8,128)(2,1)} %pad_maximum_fusion.4), calls=%async_computation.3 | async-start | bytes 2097152 | tf_op jit(solution)/shard_map/all_to_all | solution.py:44
  41.3 2.2 %copy-start.3 = (bf16[1,4,128,512]{3,2,1,0:T(8,128)(2,1)S(1)}, bf16[1,4,128,512]{3,2,1,0:T(8,128)(2,1)}, u32[]{:S(2)}) copy-start(bf16[1,4,128,512]{3,2,1,0:T(8,128)(2,1)} %get-tuple-element.12) | copy-start | bytes 1572868
  43.5 19.5 %collective-permute-start = (f32[512,4,256]{0,2,1:T(8,128)S(1)}, f32[512,4,256]{0,2,1:T(8,128)}, u32[]{:S(2)}, u32[]{:S(2)}) collective-permute-start(f32[512,4,256]{0,2,1:T(8,128)S(1)} %convolution_bitcast_fusion), channel_id=1, source_target_pairs={{0,2},{2,0},{4,6},{6,4},{8,10},{10,8},{12,14},{14,12},{16,18},{18,... | collective-permute-start | bytes 6291464 | tf_op jit(solution)/shard_map/ppermute | solution.py:8
  44.6 18.3 %all-to-all-start.2 = ((bf16[2,4,128,512]{3,2,1,0:T(8,128)(2,1)}), bf16[2,4,128,512]{3,2,1,0:T(8,128)(2,1)S(1)}, u32[]{:S(2)}, u32[]{:S(2)}) async-start(bf16[2,4,128,512]{3,2,1,0:T(8,128)(2,1)} %pad_maximum_fusion.3), calls=%async_computation.2 | async-start | bytes 2097152 | tf_op jit(solution)/shard_map/all_to_all | solution.py:44
  65.2 3.8 %copy-start.2 = (bf16[1,4,128,512]{3,2,1,0:T(8,128)(2,1)S(1)}, bf16[1,4,128,512]{3,2,1,0:T(8,128)(2,1)}, u32[]{:S(2)}) copy-start(bf16[1,4,128,512]{3,2,1,0:T(8,128)(2,1)} %get-tuple-element.13) | copy-start | bytes 1572868
  67.4 47.3 %collective-permute-start.1 = (f32[512,4,256]{0,2,1:T(8,128)S(1)}, f32[512,4,256]{0,2,1:T(8,128)}, u32[]{:S(2)}, u32[]{:S(2)}) collective-permute-start(f32[512,4,256]{0,2,1:T(8,128)S(1)} %fusion.15), channel_id=1, source_target_pairs={{0,8},{2,10},{4,12},{6,14},{8,0},{10,2},{12,4},{14,6},{16,24},{18,... | collective-permute-start | bytes 6291464 | tf_op jit(solution)/shard_map/ppermute | solution.py:8
  70.1 17.0 %all-to-all-start.1 = ((bf16[2,4,128,512]{3,2,1,0:T(8,128)(2,1)}), bf16[2,4,128,512]{3,2,1,0:T(8,128)(2,1)S(1)}, u32[]{:S(2)}, u32[]{:S(2)}) async-start(bf16[2,4,128,512]{3,2,1,0:T(8,128)(2,1)} %pad_maximum_fusion.2), calls=%async_computation.1 | async-start | bytes 2097152 | tf_op jit(solution)/shard_map/all_to_all | solution.py:44
  117.0 4.8 %copy-start.1 = (bf16[1,4,128,512]{3,2,1,0:T(8,128)(2,1)S(1)}, bf16[1,4,128,512]{3,2,1,0:T(8,128)(2,1)}, u32[]{:S(2)}) copy-start(bf16[1,4,128,512]{3,2,1,0:T(8,128)(2,1)} %get-tuple-element.14) | copy-start | bytes 1572868
  119.2 92.3 %collective-permute-start.2 = (f32[512,4,256]{0,2,1:T(8,128)S(1)}, f32[512,4,256]{0,2,1:T(8,128)}, u32[]{:S(2)}, u32[]{:S(2)}) collective-permute-start(f32[512,4,256]{0,2,1:T(8,128)S(1)} %fusion.12), channel_id=1, source_target_pairs={{0,16},{2,18},{4,20},{6,22},{8,24},{10,26},{12,28},{14,30},{16,0},... | collective-permute-start | bytes 6291464 | tf_op jit(solution)/shard_map/ppermute | solution.py:8
  122.9 16.1 %all-to-all-start = ((bf16[2,4,128,512]{3,2,1,0:T(8,128)(2,1)}), bf16[2,4,128,512]{3,2,1,0:T(8,128)(2,1)S(1)}, u32[]{:S(2)}, u32[]{:S(2)}) async-start(bf16[2,4,128,512]{3,2,1,0:T(8,128)(2,1)} %pad_maximum_fusion.1), calls=%async_computation | async-start | bytes 2097152 | tf_op jit(solution)/shard_map/all_to_all | solution.py:44
